TPU v7x, 128 devices: a whole 4x4x4 slice. The times are simulated.
128 devices in a mesh: prow: 8 (over z_hi, y), pcol: 16 (over x, z_lo, core).
Axes of the slice: x: 4, y: 4, z: 4 (z_hi: 2, z_lo: 2; z = z_hi * 2 + z_lo), core: 2. Of those that a mesh axis runs over, the one named last changes fastest.
Arguments:
- panel_t: float32 [16, 256, 8192], P('pcol', None, 'prow'), may hold values from -0.0625 to 0.0625
- ancestor: float32 [8192, 8192], P('prow', 'pcol'), as said below
- structure: int32 [16, 32], replicated, may hold values 0 or 1
- diag_inv: float32 [16, 256, 256], P('pcol'), may hold values from -6 to 6
Outputs:
- inverse_panel: float32 [4096, 8192], P('pcol', 'prow')
- inverse_diag: float32 [16, 256, 256], P('pcol')
Inputs may be any that keep to these rules, and one draw needn't show every extreme that they name: ancestor is symmetric up to rounding.
All inputs are finite; a program needn't handle non-finite values.
Results may differ from a plain program's by a relative error of at most 0.00007.
Values sent between devices are 32-bit elements; how exact they have to be, the bound alone decides.
A program may use at most 128 MiB of HBM per device.

v0:
```python
import jax
import jax.numpy as jnp
from jax import lax
from jax.sharding import PartitionSpec as P


def copy_for_each(array, axis):
    length = lax.axis_size(axis)
    return lax.all_to_all(
        jnp.broadcast_to(array[None], (length, *array.shape)), axis, 0, 0, tiled=True
    )


def of_everyone(array, axis):
    everything = copy_for_each(array, axis)
    return jnp.sum(everything, axis=0)


def local(panel_t, ancestor, structure, diag_inv):
    local_sn = panel_t.shape[0]
    width = panel_t.shape[1]
    row_span = panel_t.shape[2]
    row_blocks = row_span // width
    col_index = lax.axis_index("pcol")
    row_index = lax.axis_index("prow")
    mine = lax.dynamic_slice(
        structure, (col_index * local_sn, row_index * row_blocks), (local_sn, row_blocks)
    )
    masked = (
        panel_t.reshape(local_sn, width, row_blocks, width)
        * mine.astype(jnp.float32)[:, None, :, None]
    )
    masked = masked.reshape(local_sn, width, row_span)
    prow_size = lax.axis_size("prow")
    rows_here = width // prow_size
    arranged = masked.reshape(local_sn, prow_size, rows_here, row_span).transpose(1, 0, 2, 3)
    gathered = lax.all_gather(arranged, "pcol", axis=1, tiled=True)
    total_nodes = gathered.shape[1]
    flat_rows = gathered.reshape(prow_size * total_nodes * rows_here, row_span)
    reduced = lax.psum_scatter(
        jnp.dot(
            flat_rows, ancestor, precision=lax.Precision.HIGHEST, preferred_element_type=jnp.float32
        ),
        "prow",
        scatter_dimension=0,
        tiled=True,
    )
    moved = lax.all_to_all(
        lax.all_to_all(reduced, "pcol", split_axis=0, concat_axis=1, tiled=True),
        "prow",
        split_axis=1,
        concat_axis=0,
        tiled=True,
    )
    summed = moved.reshape(prow_size, local_sn, rows_here, row_span).transpose(1, 0, 2, 3)
    summed = summed.reshape(local_sn * width, row_span)
    inverse_panel = -summed
    blocks = inverse_panel.reshape(local_sn, width, row_span)
    partial_diag = jnp.einsum("kbj,kcj->kbc", blocks, masked, precision=lax.Precision.HIGHEST)
    inverse_diag = diag_inv - of_everyone(partial_diag, "prow")
    return (inverse_panel, inverse_diag)


def solution(mesh):
    return jax.shard_map(
        local,
        mesh=mesh,
        in_specs=(P("pcol", None, "prow"), P("prow", "pcol"), P(), P("pcol", None, None)),
        out_specs=(P("pcol", "prow"), P("pcol", None, None)),
        check_vma=False,
    )
```

profile of v0, /device:TPU:32, one launch (start us, length us, event | category | flops | bytes accessed | tf_op | source)
XLA Modules:
  0.0 340.1 jit_solution(9076834743426126464)
XLA Ops:
  7.2 0.0 copy-start
  7.2 0.0 all-gather.2.cloned.1.call-start
  7.2 0.9 convert_bitcast_fusion
  8.1 0.1 broadcast_bitcast_fusion
  8.2 2.3 broadcast_multiply_fusion
  10.6 0.0 all-gather.2.cloned.1.call-update
  10.6 0.0 reduce-scatter.2.cloned.1.call-start
  10.6 93.6 %all-gather.2.cloned.1.call-done = f32[8,16,32,1024]{3,2,1,0:T(8,128)} async-done(((f32[8,1,32,1024]{3,2,1,0:T(8,128)}), f32[8,16,32,1024]{3,2,1,0:T(8,128)}) %all-gather.2.cloned.1.call-update) | async-done | bytes 16777232 | tf_op jit(solution)/shard_map/all_gather | solution.py:37
  104.3 0.0 copy-done
  104.3 30.3 %fusion.4 = f32[4096,512]{1,0:T(8,128)} fusion(f32[4096,1024]{1,0:T(8,128)} %bitcast.27, f32[1024,512]{1,0:T(8,128)S(1)} %copy-done), kind=kOutput, calls=%fused_computation.8 | convolution fusion | flops 25769803776 | bytes 27262976 | tf_op jit(solution)/shard_map/dot_general | solution.py:41
  134.5 0.0 reduce-scatter.2.cloned.1.call-update
  134.6 0.0 copy-start.1
  134.6 114.6 %reduce-scatter.2.cloned.1.call-done = f32[512,512]{1,0:T(8,128)} async-done(((f32[4096,512]{1,0:T(8,128)}), f32[512,512]{1,0:T(8,128)}) %reduce-scatter.2.cloned.1.call-update) | async-done | bytes 1048592 | tf_op jit(solution)/shard_map/reduce_scatter | solution.py:40
  249.1 20.5 %all_to_all.34 = f32[16,32,512]{2,1,0:T(8,128)S(1)} all-to-all(f32[16,32,512]{2,1,0:T(8,128)} %bitcast.24), channel_id=1, replica_groups=mesh['prow'=8,'pcol'=16] {'pcol'}, dimensions={0} | all-to-all | bytes 2097152 | tf_op jit(solution)/shard_map/all_to_all | solution.py:49
  269.7 1.6 copy.11
  271.2 2.5 all_to_all.28
  273.8 0.0 copy-start.3
  273.8 1.9 copy.12
  275.6 21.0 %all_to_all.35 = f32[32,8,1024]{2,0,1:T(8,128)S(1)} all-to-all(f32[32,8,1024]{2,0,1:T(8,128)S(1)} %copy.12), channel_id=1, replica_groups=mesh['prow'=8,'pcol'=16] {'prow'}, dimensions={1} | all-to-all | bytes 2097152 | tf_op jit(solution)/shard_map/all_to_all | solution.py:48
  296.7 0.1 neg.13
  296.8 0.0 copy-start.2
  296.8 1.0 copy-done.2
  297.8 0.0 copy-done.1
  297.8 1.0 fusion
  298.8 0.2 broadcast_in_dim.2
  299.0 31.7 %all_to_all.36 = f32[8,1,256,256]{3,2,1,0:T(8,128)} all-to-all(f32[8,1,256,256]{3,2,1,0:T(8,128)S(1)} %broadcast_in_dim.2), channel_id=1, replica_groups=mesh['prow'=8,'pcol'=16] {'prow'}, dimensions={0} | all-to-all | bytes 4194304 | tf_op jit(solution)/shard_map/all_to_all | solution.py:9
  330.8 1.8 reduce_sum.11
  332.5 0.0 copy-done.3
  332.5 0.7 bitcast_subtract_fusion
  (1 shorter events, 0.0 us)
Async XLA Ops:
  7.2 97.1 %copy-start = (f32[1024,512]{1,0:T(8,128)S(1)}, f32[1024,512]{1,0:T(8,128)}, u32[]{:S(2)}) copy-start(f32[1024,512]{1,0:T(8,128)} %param.5) | copy-start | bytes 6291460
  7.2 97.1 %all-gather.2.cloned.1.call-start = ((), (), s32[]{:S(2)}) async-start(), calls=%async_computation.4 | async-start | bytes 17825792 | tf_op jit(solution)/shard_map/all_gather | solution.py:37
  10.6 238.6 %reduce-scatter.2.cloned.1.call-start = ((), (), s32[]{:S(2)}) async-start(), calls=%async_computation.5 | async-start | bytes 9437184 | tf_op jit(solution)/shard_map/reduce_scatter | solution.py:40
  134.6 163.2 %copy-start.1 = (f32[1,256,1024]{2,1,0:T(8,128)S(1)}, f32[1,256,1024]{2,1,0:T(8,128)}, u32[]{:S(2)}) copy-start(f32[1,256,1024]{2,1,0:T(8,128)} %param.4) | copy-start | bytes 3145732
  273.8 58.8 %copy-start.3 = (f32[1,256,256]{2,1,0:T(8,128)S(1)}, f32[1,256,256]{2,1,0:T(8,128)}, u32[]{:S(2)}) copy-start(f32[1,256,256]{2,1,0:T(8,128)} %param.7) | copy-start | bytes 786436
  296.8 1.0 copy-start.2
Sparse Core Ops, SparseCore 0:
  10.7 93.5 all-gather.1
  134.7 114.4 reduce-scatter.1
where the time goes:
time: 340 us
  waiting for transfers between devices  208 us (61%)
  blocking collectives  73.3 us (22%)
  matrix products  31.3 us (9%)
  between operations  14.1 us (4%)
  local copies, waits for them, and re-layouts  7.22 us (2%)
  other arithmetic  5.85 us (2%)
    reduce_scatter x1, waiting for transfers between devices, local(): lax.psum_scatter(jnp.dot(flat_rows, ancestor, precision=lax.Precision.HIG...  115 us
    all_gather x1, waiting for transfers between devices, local(): gathered = lax.all_gather(arranged, 'pcol', axis=1, tiled=True)  93.6 us
    all_to_all x1, blocking collectives, copy_for_each(): lax.all_to_all(jnp.broadcast_to(array[None], (length, *array.shape)), axi...  31.7 us
    dot_general x1, matrix products, local(): jnp.dot(flat_rows, ancestor, precision=lax.Precision.HIGHEST, preferred_e...  30.3 us
    all_to_all x1, blocking collectives, local(): lax.all_to_all(lax.all_to_all(reduced, 'pcol', split_axis=0, concat_axis=...  21 us
    all_to_all x1, blocking collectives, local(): lax.all_to_all(reduced, 'pcol', split_axis=0, concat_axis=1, tiled=True)  20.5 us
  transfers between devices with their start and end apart: 2, of which 2 were waited for; matrix products, arithmetic and copies ran while one was open for 0% of the time, Pallas kernels for 0%

commit v1 on v0

--- a/solution.py
+++ b/solution.py
@@ -34,7 +34,9 @@
     prow_size = lax.axis_size("prow")
     rows_here = width // prow_size
     arranged = masked.reshape(local_sn, prow_size, rows_here, row_span).transpose(1, 0, 2, 3)
-    gathered = lax.all_gather(arranged, "pcol", axis=1, tiled=True)
+    gathered = jnp.concatenate(
+        lax.all_to_all(jnp.stack([arranged] * lax.axis_size("pcol")), "pcol", 0, 0), axis=1
+    )
     total_nodes = gathered.shape[1]
     flat_rows = gathered.reshape(prow_size * total_nodes * rows_here, row_span)
     reduced = lax.psum_scatter(

time: 340 us -> 441 us (1.30)
  blocking collectives: 73.3 us -> 262 us
  waiting for transfers between devices: 208 us -> 116 us
  local copies, waits for them, and re-layouts: 7.22 us -> 12.6 us
    all_to_all x0 -> x1, blocking collectives: none -> 189 us  [local(): lax.all_to_all(jnp.stack([arranged] * lax.axis_size('pcol')), 'pcol', 0, 0)]
    all_gather x1 -> x0, waiting for transfers between devices: 93.6 us -> none  [local(): gathered = lax.all_gather(arranged, 'pcol', axis=1, tiled=True)]
  transfers between devices with their start and end apart: 2 -> 1, of which waited for: 2 -> 1; matrix products, arithmetic and copies ran while one was open for 0% -> 0% of each run, Pallas kernels for 0% -> 0%
where the time goes in v1:
time: 441 us
  blocking collectives  262 us (59%)
  waiting for transfers between devices  116 us (26%)
  matrix products  29.7 us (7%)
  between operations  14.1 us (3%)
  local copies, waits for them, and re-layouts  12.6 us (3%)
  other arithmetic  5.85 us (1%)
    all_to_all x1, blocking collectives, local(): lax.all_to_all(jnp.stack([arranged] * lax.axis_size('pcol')), 'pcol', 0, 0)  189 us
    reduce_scatter x1, waiting for transfers between devices, local(): lax.psum_scatter(jnp.dot(flat_rows, ancestor, precision=lax.Precision.HIG...  116 us
    all_to_all x1, blocking collectives, copy_for_each(): lax.all_to_all(jnp.broadcast_to(array[None], (length, *array.shape)), axi...  31.7 us
    dot_general x1, matrix products, local(): jnp.dot(flat_rows, ancestor, precision=lax.Precision.HIGHEST, preferred_e...  28.6 us
    all_to_all x1, blocking collectives, local(): lax.all_to_all(lax.all_to_all(reduced, 'pcol', split_axis=0, concat_axis=...  21 us
    all_to_all x1, blocking collectives, local(): lax.all_to_all(reduced, 'pcol', split_axis=0, concat_axis=1, tiled=True)  20.5 us
  transfers between devices with their start and end apart: 1, of which 1 were waited for; matrix products, arithmetic and copies ran while one was open for 0% of the time, Pallas kernels for 0%

profile of v1, /device:TPU:32, one launch (start us, length us, event | category | flops | bytes accessed | tf_op | source)
XLA Modules:
  0.0 440.7 jit_solution(8418309956856110937)
XLA Ops:
  7.2 0.0 copy-start
  7.2 0.0 reduce-scatter.2.cloned.1.call-start
  7.2 0.9 convert_bitcast_fusion
  8.1 0.1 broadcast_bitcast_fusion
  8.2 2.3 broadcast_multiply_fusion
  10.6 3.4 stack.3
  14.0 188.9 %all_to_all.39 = f32[16,8,1,32,1024]{4,3,1,2,0:T(8,128)S(1)} all-to-all(f32[16,8,1,32,1024]{4,3,1,2,0:T(8,128)S(1)} %stack.3), channel_id=1, replica_groups=mesh['prow'=8,'pcol'=16] {'pcol'}, dimensions={0} | all-to-all | bytes 33554432 | tf_op jit(solution)/shard_map/all_to_all | solution.py:38
  202.9 1.9 copy.12
  204.8 0.0 copy-done
  204.8 28.6 %fusion.4 = f32[4096,512]{1,0:T(8,128)} fusion(f32[4096,1024]{1,0:T(8,128)S(1)} %bitcast.22, f32[1024,512]{1,0:T(8,128)S(1)} %copy-done), kind=kOutput, calls=%fused_computation.8 | convolution fusion | flops 25769803776 | bytes 27262976 | tf_op jit(solution)/shard_map/dot_general | solution.py:43
  233.4 0.0 reduce-scatter.2.cloned.1.call-update
  233.5 0.0 copy-start.1
  233.5 116.2 %reduce-scatter.2.cloned.1.call-done = f32[512,512]{1,0:T(8,128)} async-done(((f32[4096,512]{1,0:T(8,128)}), f32[512,512]{1,0:T(8,128)}) %reduce-scatter.2.cloned.1.call-update) | async-done | bytes 1048592 | tf_op jit(solution)/shard_map/reduce_scatter | solution.py:42
  349.7 20.5 %all_to_all.40 = f32[16,32,512]{2,1,0:T(8,128)S(1)} all-to-all(f32[16,32,512]{2,1,0:T(8,128)} %bitcast.27), channel_id=1, replica_groups=mesh['prow'=8,'pcol'=16] {'pcol'}, dimensions={0} | all-to-all | bytes 2097152 | tf_op jit(solution)/shard_map/all_to_all | solution.py:51
  370.2 1.6 copy.13
  371.8 2.5 all_to_all.32
  374.4 0.0 copy-start.3
  374.4 1.9 copy.14
  376.2 21.0 %all_to_all.41 = f32[32,8,1024]{2,0,1:T(8,128)S(1)} all-to-all(f32[32,8,1024]{2,0,1:T(8,128)S(1)} %copy.14), channel_id=1, replica_groups=mesh['prow'=8,'pcol'=16] {'prow'}, dimensions={1} | all-to-all | bytes 2097152 | tf_op jit(solution)/shard_map/all_to_all | solution.py:50
  397.2 0.1 neg.13
  397.4 0.0 copy-start.2
  397.4 1.0 copy-done.2
  398.3 0.0 copy-done.1
  398.3 1.0 fusion
  399.4 0.2 broadcast_in_dim.2
  399.6 31.7 %all_to_all.42 = f32[8,1,256,256]{3,2,1,0:T(8,128)} all-to-all(f32[8,1,256,256]{3,2,1,0:T(8,128)S(1)} %broadcast_in_dim.2), channel_id=1, replica_groups=mesh['prow'=8,'pcol'=16] {'prow'}, dimensions={0} | all-to-all | bytes 4194304 | tf_op jit(solution)/shard_map/all_to_all | solution.py:9
  431.3 1.8 reduce_sum.11
  433.1 0.0 copy-done.3
  433.1 0.7 bitcast_subtract_fusion
  (1 shorter events, 0.0 us)
Async XLA Ops:
  7.2 197.6 %copy-start = (f32[1024,512]{1,0:T(8,128)S(1)}, f32[1024,512]{1,0:T(8,128)}, u32[]{:S(2)}) copy-start(f32[1024,512]{1,0:T(8,128)} %param.5) | copy-start | bytes 6291460
  7.2 342.5 %reduce-scatter.2.cloned.1.call-start = ((), (), s32[]{:S(2)}) async-start(), calls=%async_computation.5 | async-start | bytes 9437184 | tf_op jit(solution)/shard_map/reduce_scatter | solution.py:42
  233.5 164.9 %copy-start.1 = (f32[1,256,1024]{2,1,0:T(8,128)S(1)}, f32[1,256,1024]{2,1,0:T(8,128)}, u32[]{:S(2)}) copy-start(f32[1,256,1024]{2,1,0:T(8,128)} %param.4) | copy-start | bytes 3145732
  374.4 58.7 %copy-start.3 = (f32[1,256,256]{2,1,0:T(8,128)S(1)}, f32[1,256,256]{2,1,0:T(8,128)}, u32[]{:S(2)}) copy-start(f32[1,256,256]{2,1,0:T(8,128)} %param.7) | copy-start | bytes 786436
  397.4 1.0 copy-start.2
Sparse Core Ops, SparseCore 0:
  233.6 116.0 reduce-scatter.1
